TPU v7x, 32 devices: a whole 2x2x4 slice. The times are simulated.
32 devices in a mesh: orb: 8 (over y, x, core), walk: 4 (over z).
Axes of the slice: x: 2, y: 2, z: 4, core: 2. Of those that a mesh axis runs over, the one named last changes fastest.
Arguments:
- chol: bfloat16 [32, 2048, 2048], P(None, 'orb', 'walk'), may hold values from -6 to 6
- orbitals: bfloat16 [2048, 1024], replicated, may hold values from -0.125 to 0.125
- greens: bfloat16 [4, 1024, 2048], P('walk'), may hold values from -0.00390625 to 0.00390625
- shift: float32 [32], P('orb'), may hold values from -6 to 6
Outputs:
- force_bias: float32 [4, 32], P('walk', 'orb')
- rotated: bfloat16 [32, 1024, 2048], P('orb', None, 'walk')
All inputs are finite; a program needn't handle non-finite values.
Results may differ from a plain program's by a relative error of at most 0.007.
Values may be sent and summed in bfloat16 or wider, within the bound.
A program may use at most 64 MiB of HBM per device.

v0:
```python
import jax
import jax.numpy as jnp
from jax import lax
from jax.sharding import PartitionSpec as P


def local(chol, orbitals, greens, shift):
    regrouped = lax.all_to_all(chol, "orb", split_axis=0, concat_axis=1, tiled=True)
    rotation = jnp.einsum("pi,gpq->giq", orbitals, regrouped, preferred_element_type=jnp.float32)
    rotated = rotation.astype(jnp.bfloat16)
    row_count = chol.shape[1]
    row_start = lax.axis_index("orb") * row_count
    orbital_rows = lax.dynamic_slice_in_dim(orbitals, row_start, row_count, 0)
    products = jnp.einsum("pi,wiq->wpq", orbital_rows, greens, preferred_element_type=jnp.float32)
    arrived = lax.all_to_all(
        products.astype(jnp.bfloat16), "walk", split_axis=2, concat_axis=0, tiled=True
    ).astype(products.dtype)
    terms = jnp.einsum(
        "wpq,gpq->wg", arrived, chol.astype(jnp.float32), precision=lax.Precision.HIGHEST
    )
    by_vector = lax.psum_scatter(terms, "orb", scatter_dimension=1, tiled=True)
    totals = lax.psum_scatter(by_vector, "walk", scatter_dimension=0, tiled=True)
    return (totals - shift[None, :], rotated)


def solution(mesh):
    in_specs = (P(None, "orb", "walk"), P(), P("walk", None, None), P("orb"))
    out_specs = (P("walk", "orb"), P("orb", None, "walk"))
    return jax.shard_map(local, mesh=mesh, in_specs=in_specs, out_specs=out_specs, check_vma=False)
```

profile of v0, /device:TPU:0, one launch (start us, length us, event | category | flops | bytes accessed | tf_op | source)
XLA Modules:
  0.0 214.4 jit_solution(16381867713157282100)
XLA Ops:
  0.6 3.6 %fusion.11 = bf16[1,256,2048]{2,1,0:T(8,128)(2,1)S(1)} fusion(bf16[1,1024,2048]{2,1,0:T(8,128)(2,1)} %param.6, bf16[2048,1024]{1,0:T(8,128)(2,1)} %param.5, s32[]{:T(128)S(6)} %select_n.3), kind=kOutput, calls=%fused_computation.8 | convolution fusion | flops 1074266112 | bytes 5767172 | tf_op jit(solution)/shard_map/pi,wiq->wpq/dot_general | solution.py:14
  4.3 1.7 copy.9
  5.9 0.5 broadcast
  6.5 10.6 %reduce = bf16[2048,256]{1,0:T(8,128)(2,1)S(1)} reduce(bf16[2048,1,256]{2,1,0:T(2,128)(2,1)S(1)} %bitcast.45, bf16[]{:T(256)} %broadcast), dimensions={1}, to_apply=%bitcast.40.reduce_sub_computation | reduce | bytes 2097154
  17.1 0.3 reshape.17
  17.4 31.9 %all_to_all.36 = bf16[4,2,65536]{2,1,0:T(2,128)(2,1)S(1)} all-to-all(bf16[4,2,65536]{2,1,0:T(2,128)(2,1)S(1)} %reshape.17), channel_id=1, replica_groups=mesh['orb'=8,'walk'=4] {'walk'}, dimensions={0} | all-to-all | bytes 2097152 | tf_op jit(solution)/shard_map/all_to_all | solution.py:15
  49.3 0.0 copy-start.2
  49.3 0.0 copy-start.1
  49.3 5.4 %all-to-all-start.1 = ((bf16[32,256,512]{2,1,0:T(8,128)(2,1)}), bf16[32,256,512]{2,1,0:T(8,128)(2,1)}, u32[]{:S(2)}, u32[]{:S(2)}) async-start(bf16[32,256,512]{2,1,0:T(8,128)(2,1)} %param.4), calls=%async_computation.1 | async-start | bytes 16777216 | tf_op jit(solution)/shard_map/all_to_all | solution.py:8
  54.6 0.0 copy-done.2
  54.7 0.6 dynamic-slice
  55.2 0.0 copy-done.1
  55.2 0.6 dynamic-slice.2
  56.5 1.0 reshape.18
  57.5 0.2 copy.16
  57.6 1.0 copy.14
  58.7 0.0 copy-start
  58.7 13.1 %fusion.14 = f32[4,32]{1,0:T(4,128)S(1)} fusion(bf16[32,256,512]{2,1,0:T(8,128)(2,1)} %param.4, bf16[1,256,4,512]{3,2,1,0:T(4,128)(2,1)S(1)} %copy.14), kind=kOutput, calls=%fused_computation.9 | convolution fusion | flops 33554432 | bytes 9437696 | tf_op jit(solution)/shard_map/wpq,gpq->wg/dot_general | solution.py:18
  71.7 83.1 %all-reduce = f32[4,32]{1,0:T(4,128)S(1)} all-reduce(f32[4,32]{1,0:T(4,128)S(1)} %fusion.14), channel_id=2, replica_groups=mesh['orb'=8,'walk'=4] {'orb'}, use_global_device_ids=true, to_apply=%region_0.0.clone | all-reduce | flops 128 | bytes 1024
  154.9 0.1 constant_dynamic-slice_fusion.1
  154.9 10.0 %all-reduce.1 = f32[4,4]{1,0:T(4,128)S(1)} all-reduce(f32[4,4]{1,0:T(4,128)S(1)} %constant_dynamic-slice_fusion.1), channel_id=3, replica_groups=mesh['orb'=8,'walk'=4] {'walk'}, use_global_device_ids=true, to_apply=%region_1.0.clone | all-reduce | flops 16 | bytes 128
  164.9 0.0 copy-done
  164.9 1.2 fusion.19
  166.1 0.0 all-to-all-done.1
  166.1 14.8 %copy.12 = bf16[8,4,256,512]{2,0,3,1:T(8,128)(2,1)} copy(bf16[8,4,256,512]{3,2,1,0:T(8,128)(2,1)} %bitcast.8) | data formatting | bytes 16777216 | tf_op jit(solution)/shard_map/all_to_all | solution.py:8
  180.9 13.5 %all_to_all.33 = bf16[4,2048,512]{1,2,0:T(8,128)(2,1)} reshape(bf16[4,8,256,512]{2,1,3,0:T(8,128)(2,1)} %bitcast.43) | data formatting | bytes 16777216 | tf_op jit(solution)/shard_map/all_to_all | solution.py:8
  194.4 13.8 %convert_bitcast_fusion = bf16[4,1024,512]{1,2,0:T(8,128)(2,1)} fusion(bf16[4,2048,512]{1,2,0:T(8,128)(2,1)} %all_to_all.33, bf16[2048,1024]{1,0:T(8,128)(2,1)} %param.5), kind=kOutput, calls=%fused_computation.6 | convolution fusion | flops 8592031744 | bytes 16777216 | tf_op jit(solution)/shard_map/pi,gpq->giq/dot_general | solution.py:9
  208.2 6.2 %copy.13 = bf16[4,1024,512]{2,1,0:T(8,128)(2,1)} copy(bf16[4,1024,512]{1,2,0:T(8,128)(2,1)} %convert_bitcast_fusion) | data formatting | bytes 8388608
Async XLA Ops:
  49.3 5.4 %copy-start.2 = (u32[32]{0:T(128)S(1)}, u32[32]{0:T(128)}, u32[]{:S(2)}) copy-start(u32[32]{0:T(128)} %constant.16) | copy-start | bytes 388
  49.3 6.0 %copy-start.1 = (u32[32]{0:T(128)S(1)}, u32[32]{0:T(128)}, u32[]{:S(2)}) copy-start(u32[32]{0:T(128)} %constant.20) | copy-start | bytes 388
  49.3 116.8 %all-to-all-start.1 = ((bf16[32,256,512]{2,1,0:T(8,128)(2,1)}), bf16[32,256,512]{2,1,0:T(8,128)(2,1)}, u32[]{:S(2)}, u32[]{:S(2)}) async-start(bf16[32,256,512]{2,1,0:T(8,128)(2,1)} %param.4), calls=%async_computation.1 | async-start | bytes 16777216 | tf_op jit(solution)/shard_map/all_to_all | solution.py:8
  58.7 106.3 %copy-start = (f32[4]{0:T(128)S(1)}, f32[4]{0:T(128)}, u32[]{:S(2)}) copy-start(f32[4]{0:T(128)} %param.7) | copy-start | bytes 52
where the time goes:
time: 215 us; the launch traced here: 214 us
  blocking collectives  125 us (58%)
  local copies, waits for them, and re-layouts  40.4 us (19%)
  matrix products  30.5 us (14%)
  other arithmetic  11.8 us (5%)
  starting transfers between devices  5.36 us (2%)
    unnamed x2, blocking collectives  93.1 us
    all_to_all x1, blocking collectives, local(): lax.all_to_all(products.astype(jnp.bfloat16), 'walk', split_axis=2, conca...  31.9 us
    all_to_all x2, local copies, waits for them, and re-layouts, local(): lax.all_to_all(chol, 'orb', split_axis=0, concat_axis=1, tiled=True)  28.3 us
    dot_general x1, matrix products, local(): jnp.einsum('pi,gpq->giq', orbitals, regrouped, preferred_element_type=jnp...  13.8 us
    dot_general x1, matrix products, local(): jnp.einsum('wpq,gpq->wg', arrived, chol.astype(jnp.float32), precision=la...  13.1 us
    unnamed x1, other arithmetic  10.6 us
    unnamed x14, local copies, waits for them, and re-layouts  9.43 us
    all_to_all x1, starting transfers between devices, local(): lax.all_to_all(chol, 'orb', split_axis=0, concat_axis=1, tiled=True)  5.36 us
  transfers between devices with their start and end apart: 1, of which 0 were waited for; matrix products, arithmetic and copies ran while one was open for 8% of the time, Pallas kernels for 0%

commit v1 on v0

--- a/solution.py
+++ b/solution.py
@@ -12,8 +12,14 @@
     row_start = lax.axis_index("orb") * row_count
     orbital_rows = lax.dynamic_slice_in_dim(orbitals, row_start, row_count, 0)
     products = jnp.einsum("pi,wiq->wpq", orbital_rows, greens, preferred_element_type=jnp.float32)
-    arrived = lax.all_to_all(
-        products.astype(jnp.bfloat16), "walk", split_axis=2, concat_axis=0, tiled=True
+    arrived = jnp.concatenate(
+        lax.all_to_all(
+            jnp.stack(jnp.split(products.astype(jnp.bfloat16), lax.axis_size("walk"), axis=2)),
+            "walk",
+            0,
+            0,
+        ),
+        axis=0,
     ).astype(products.dtype)
     terms = jnp.einsum(
         "wpq,gpq->wg", arrived, chol.astype(jnp.float32), precision=lax.Precision.HIGHEST

time: 215 us -> 203 us (0.944)
  other arithmetic: 11.8 us -> 1.3 us
  local copies, waits for them, and re-layouts: 40.4 us -> 35.8 us
    unnamed x1 -> x0, other arithmetic: 10.6 us -> none
    unnamed x14 -> x10, local copies, waits for them, and re-layouts: 9.43 us -> 7.44 us
where the time goes in v1:
time: 203 us; the launch traced here: 201 us
  blocking collectives  127 us (63%)
  local copies, waits for them, and re-layouts  35.8 us (18%)
  matrix products  31 us (15%)
  starting transfers between devices  5.17 us (3%)
    unnamed x2, blocking collectives  94.9 us
    all_to_all x1, blocking collectives, local(): lax.all_to_all(jnp.stack(jnp.split(products.astype(jnp.bfloat16), lax.axi...  31.9 us
    all_to_all x2, local copies, waits for them, and re-layouts, local(): lax.all_to_all(chol, 'orb', split_axis=0, concat_axis=1, tiled=True)  28.3 us
    dot_general x1, matrix products, local(): jnp.einsum('pi,gpq->giq', orbitals, regrouped, preferred_element_type=jnp...  13.8 us
    dot_general x1, matrix products, local(): jnp.einsum('wpq,gpq->wg', arrived, chol.astype(jnp.float32), precision=la...  13.6 us
    unnamed x10, local copies, waits for them, and re-layouts  7.44 us
    all_to_all x1, starting transfers between devices, local(): lax.all_to_all(chol, 'orb', split_axis=0, concat_axis=1, tiled=True)  5.17 us
  transfers between devices with their start and end apart: 1, of which 0 were waited for; matrix products, arithmetic and copies ran while one was open for 8% of the time, Pallas kernels for 0%

profile of v1, /device:TPU:0, one launch (start us, length us, event | category | flops | bytes accessed | tf_op | source)
XLA Modules:
  0.0 201.4 jit_solution(7926491329529676716)
XLA Ops:
  0.6 3.6 %fusion.11 = bf16[1,256,2048]{2,1,0:T(8,128)(2,1)S(1)} fusion(bf16[1,1024,2048]{2,1,0:T(8,128)(2,1)} %param.6, bf16[2048,1024]{1,0:T(8,128)(2,1)} %param.5, s32[]{:T(128)S(6)} %select_n.3), kind=kOutput, calls=%fused_computation.8 | convolution fusion | flops 1074266112 | bytes 5767172 | tf_op jit(solution)/shard_map/pi,wiq->wpq/dot_general | solution.py:14
  4.3 0.1 slice_bitcast_fusion.3
  4.3 0.1 pad_maximum_fusion
  4.5 31.9 %all_to_all.23 = bf16[4,1,256,512]{3,2,1,0:T(8,128)(2,1)S(1)} all-to-all(bf16[4,1,256,512]{3,2,1,0:T(8,128)(2,1)S(1)} %pad_maximum_fusion), channel_id=1, replica_groups=mesh['orb'=8,'walk'=4] {'walk'}, dimensions={0} | all-to-all | bytes 2097152 | tf_op jit(solution)/shard_map/all_to_all | solution.py:16
  36.4 0.0 copy-start.2
  36.4 0.0 copy-start.1
  36.4 5.2 %all-to-all-start.1 = ((bf16[32,256,512]{2,1,0:T(8,128)(2,1)}), bf16[32,256,512]{2,1,0:T(8,128)(2,1)}, u32[]{:S(2)}, u32[]{:S(2)}) async-start(bf16[32,256,512]{2,1,0:T(8,128)(2,1)} %param.4), calls=%async_computation.1 | async-start | bytes 16777216 | tf_op jit(solution)/shard_map/all_to_all | solution.py:8
  41.5 0.0 copy-done.2
  41.6 0.6 dynamic-slice
  42.1 0.0 copy-done.1
  42.1 0.6 dynamic-slice.2
  43.4 0.0 copy-start
  43.4 13.6 %fusion.14 = f32[4,32]{1,0:T(4,128)S(1)} fusion(bf16[32,256,512]{2,1,0:T(8,128)(2,1)} %param.4, bf16[4,256,512]{2,1,0:T(8,128)(2,1)S(1)} %bitcast.45), kind=kOutput, calls=%fused_computation.9 | convolution fusion | flops 33554432 | bytes 9437696 | tf_op jit(solution)/shard_map/wpq,gpq->wg/dot_general | solution.py:24
  57.0 84.9 %all-reduce = f32[4,32]{1,0:T(4,128)S(1)} all-reduce(f32[4,32]{1,0:T(4,128)S(1)} %fusion.14), channel_id=2, replica_groups=mesh['orb'=8,'walk'=4] {'orb'}, use_global_device_ids=true, to_apply=%region_0.0.clone | all-reduce | flops 128 | bytes 1024
  141.9 0.1 constant_dynamic-slice_fusion.1
  142.0 10.0 %all-reduce.1 = f32[4,4]{1,0:T(4,128)S(1)} all-reduce(f32[4,4]{1,0:T(4,128)S(1)} %constant_dynamic-slice_fusion.1), channel_id=3, replica_groups=mesh['orb'=8,'walk'=4] {'walk'}, use_global_device_ids=true, to_apply=%region_1.0.clone | all-reduce | flops 16 | bytes 128
  152.0 0.0 copy-done
  152.0 1.2 fusion.19
  153.2 0.0 all-to-all-done.1
  153.2 14.8 %copy.12 = bf16[8,4,256,512]{2,0,3,1:T(8,128)(2,1)} copy(bf16[8,4,256,512]{3,2,1,0:T(8,128)(2,1)} %bitcast.13) | data formatting | bytes 16777216 | tf_op jit(solution)/shard_map/all_to_all | solution.py:8
  168.0 13.5 %all_to_all.20 = bf16[4,2048,512]{1,2,0:T(8,128)(2,1)} reshape(bf16[4,8,256,512]{2,1,3,0:T(8,128)(2,1)} %bitcast.44) | data formatting | bytes 16777216 | tf_op jit(solution)/shard_map/all_to_all | solution.py:8
  181.4 13.8 %convert_bitcast_fusion = bf16[4,1024,512]{1,2,0:T(8,128)(2,1)} fusion(bf16[4,2048,512]{1,2,0:T(8,128)(2,1)} %all_to_all.20, bf16[2048,1024]{1,0:T(8,128)(2,1)} %param.5), kind=kOutput, calls=%fused_computation.6 | convolution fusion | flops 8592031744 | bytes 16777216 | tf_op jit(solution)/shard_map/pi,gpq->giq/dot_general | solution.py:9
  195.2 6.2 %copy.13 = bf16[4,1024,512]{2,1,0:T(8,128)(2,1)} copy(bf16[4,1024,512]{1,2,0:T(8,128)(2,1)} %convert_bitcast_fusion) | data formatting | bytes 8388608
Async XLA Ops:
  36.4 5.2 %copy-start.2 = (u32[32]{0:T(128)S(1)}, u32[32]{0:T(128)}, u32[]{:S(2)}) copy-start(u32[32]{0:T(128)} %constant.16) | copy-start | bytes 388
  36.4 5.8 %copy-start.1 = (u32[32]{0:T(128)S(1)}, u32[32]{0:T(128)}, u32[]{:S(2)}) copy-start(u32[32]{0:T(128)} %constant.20) | copy-start | bytes 388
  36.4 116.8 %all-to-all-start.1 = ((bf16[32,256,512]{2,1,0:T(8,128)(2,1)}), bf16[32,256,512]{2,1,0:T(8,128)(2,1)}, u32[]{:S(2)}, u32[]{:S(2)}) async-start(bf16[32,256,512]{2,1,0:T(8,128)(2,1)} %param.4), calls=%async_computation.1 | async-start | bytes 16777216 | tf_op jit(solution)/shard_map/all_to_all | solution.py:8
  43.4 108.6 %copy-start = (f32[4]{0:T(128)S(1)}, f32[4]{0:T(128)}, u32[]{:S(2)}) copy-start(f32[4]{0:T(128)} %param.7) | copy-start | bytes 52
